TPU v7x, 32 devices: a whole 2x2x4 slice. The times are simulated.
32 devices in a mesh: grp: 2 (over x), col: 8 (over z, core), lay: 2 (over y).
Axes of the slice: x: 2, y: 2, z: 4, core: 2. Of those that a mesh axis runs over, the one named last changes fastest.
Arguments:
- gradient: float32 [2, 2, 24, 6144, 128], P('grp', 'lay', None, 'col'), may hold values from -410 to 410
- momentum: float32 [2, 2, 24, 6144, 128], P('grp', 'lay', None, 'col'), may hold values from -820 to 820
- probe_vector: float32 [128], replicated, may hold values from -4 to 4
Outputs:
- new_momentum: float32 [2, 2, 24, 6144, 128], P('grp', 'lay', None, 'col')
- update: float32 [2, 2, 24, 6144, 128], P('grp', 'lay', None, 'col')
All inputs are finite; a program needn't handle non-finite values.
Results may differ from a plain program's by a relative error of at most 0.00022.
Values sent between devices are 32-bit elements; how exact they have to be, the bound alone decides.
No kernel may reach another device: no remote copies, remote signals or barrier semaphores. Data moves between devices by JAX's collectives and lax.ppermute only.
A program may use at most 128 MiB of HBM per device.

v0:
```python
import math

import jax
import jax.numpy as jnp
from jax import lax
from jax.sharding import PartitionSpec as P

D = 6144
ITERS = 3


MOMENTUM_DECAY = 0.95
LINEAR_TERM = 3.4445
CUBIC_TERM = -4.775
QUINTIC_TERM = 2.0315
EPSILON = 1e-06
PRECISE = lax.Precision.HIGHEST


def summed_gram(stack):
    partial_gram = jnp.einsum("glhdr,glhds->glhrs", stack, stack, precision=PRECISE)
    return lax.psum(partial_gram, "col")


def head_bound(product, probe_norm):
    estimate = jnp.sqrt(jnp.sum(product * product, axis=-1) + EPSILON) / probe_norm
    local_most = jnp.max(estimate, axis=(0, 1))
    overall = lax.pmax(local_most, ("grp", "lay"))
    return 2.0 * jnp.sqrt(overall)


def on_device(gradient, momentum, probe_vector):
    new_momentum = MOMENTUM_DECAY * momentum + gradient
    blend = gradient + MOMENTUM_DECAY * new_momentum
    width = blend.shape[-1]
    probe_norm = jnp.sqrt(jnp.sum(probe_vector * probe_vector) + EPSILON)
    raw_gram = summed_gram(blend)
    product = jnp.einsum("glhrs,s->glhr", raw_gram, probe_vector, precision=PRECISE)
    bound_value = head_bound(product, probe_norm)
    scaled = blend / bound_value[None, None, :, None, None]
    current = raw_gram / (bound_value * bound_value)[None, None, :, None, None]
    identity = jnp.eye(width, dtype=jnp.float32)
    total = jnp.broadcast_to(identity, current.shape)
    for counter in range(ITERS):
        square = jnp.einsum("glhrs,glhst->glhrt", current, current, precision=PRECISE)
        mixing = LINEAR_TERM * identity + CUBIC_TERM * current + QUINTIC_TERM * square
        total = jnp.einsum("glhrs,glhst->glhrt", total, mixing, precision=PRECISE)
        if counter + 1 < ITERS:
            halfway = jnp.einsum("glhrs,glhst->glhrt", mixing, current, precision=PRECISE)
            current = jnp.einsum("glhrs,glhst->glhrt", halfway, mixing, precision=PRECISE)
    polished = jnp.einsum("glhdr,glhrs->glhds", scaled, total, precision=PRECISE)
    update = polished * (0.2 * math.sqrt(D))
    return (new_momentum, update)


def solution(mesh):
    in_specs = (P("grp", "lay", None, "col", None), P("grp", "lay", None, "col", None), P())
    out_specs = (P("grp", "lay", None, "col", None), P("grp", "lay", None, "col", None))
    return jax.shard_map(
        on_device, mesh=mesh, in_specs=in_specs, out_specs=out_specs, check_vma=False
    )
```

profile of v0, /device:TPU:0, one launch (start us, length us, event | category | flops | bytes accessed | tf_op | source)
XLA Modules:
  0.0 162.3 jit_solution(10926613362764965501)
XLA Ops:
  7.2 0.0 all-reduce.2.cloned.1.call-start
  7.2 11.6 %multiply_add_fusion.1 = f32[1,1,24,768,128]{4,3,2,1,0:T(8,128)} fusion(f32[1,1,24,768,128]{4,3,2,1,0:T(8,128)} %param.3, f32[1,1,24,768,128]{4,3,2,1,0:T(8,128)} %param.4), kind=kLoop, calls=%fused_computation.7 | loop fusion | flops 4718592 | bytes 28311552 | tf_op jit(solution)/shard_map/add | solution.py:33
  18.8 29.0 %fusion.30 = f32[1,1,24,128,128]{4,3,2,1,0:T(8,128)} fusion(f32[1,1,24,768,128]{4,3,2,1,0:T(8,128)} %param.3, f32[1,1,24,768,128]{4,3,2,1,0:T(8,128)} %multiply_add_fusion.1), kind=kOutput, calls=%fused_computation.33 | convolution fusion | flops 3628597248 | bytes 20447232 | tf_op jit(solution)/shard_map/glhdr,glhds->glhrs/dot_general | solution.py:21
  47.8 0.0 copy-start.1
  47.8 0.0 all-reduce.2.cloned.1.call-update
  47.8 0.6 copy-done.1
  48.4 0.7 multiply_reduce_fusion.1
  49.8 62.7 %all-reduce.2.cloned.1.call-done = f32[1,1,24,128,128]{4,3,2,1,0:T(8,128)} async-done(((f32[1,1,24,128,128]{4,3,2,1,0:T(8,128)}), f32[1,1,24,128,128]{4,3,2,1,0:T(8,128)}) %all-reduce.2.cloned.1.call-update) | async-done | bytes 1572880 | tf_op jit(solution)/shard_map/psum | solution.py:22
  112.5 0.0 copy-start
  112.5 2.9 %fusion.17 = f32[1,24,128]{2,0,1:T(1,128)S(1)} fusion(f32[1,1,24,128,128]{4,3,2,1,0:T(8,128)} %all-reduce.2.cloned.1.call-done, f32[128]{0:T(128)S(1)} %copy-done.1), kind=kOutput, calls=%fused_computation.19 | convolution fusion | flops 4718592 | bytes 1585664 | tf_op jit(solution)/shard_map/glhrs,s->glhr/dot_general | solution.py:38
  115.5 0.1 multiply_reduce_fusion
  115.6 9.8 %pmax.7 = f32[24]{0:T(128)S(1)} all-reduce(f32[24]{0:T(128)S(1)} %sqrt_divide_fusion), channel_id=1, replica_groups=mesh['grp'=2,'col'=8,'lay'=2] {'grp','lay'}, use_global_device_ids=true, to_apply=%region_3.0 | all-reduce | flops 24 | bytes 192 | tf_op jit(solution)/shard_map/pmax | solution.py:28
  125.4 0.0 copy-done
  125.4 2.1 %bitcast_add_fusion = f32[1,1,24,128,128]{4,3,2,1,0:T(8,128)S(1)} fusion(f32[128,128]{1,0:T(8,128)S(1)} %fusion.48, f32[1,1,24,128,128]{4,3,2,1,0:T(8,128)S(1)} %copy-done, f32[24]{0:T(128)S(1)} %get-tuple-element.3), kind=kOutput, calls=%fused_computation.15 | convolution fusion | flops 606339072 | bytes 3211360 | tf_op jit(solution)/shard_map/glhrs,glhst->glhrt/dot_general | solution.py:45
  127.5 1.8 %fusion.10 = f32[24,128,128]{2,1,0:T(8,128)S(1)} fusion(f32[1,1,24,128,128]{4,3,2,1,0:T(8,128)S(1)} %bitcast_add_fusion, f32[1,1,24,128,128]{4,3,2,1,0:T(8,128)S(1)} %copy-done, f32[24]{0:T(128)S(1)} %get-tuple-element.3), kind=kOutput, calls=%fused_computation.11 | convolution fusion | flops 604372992 | bytes 4718688 | tf_op jit(solution)/shard_map/glhrs,glhst->glhrt/dot_general | solution.py:49
  129.3 1.7 %fusion.8 = f32[24,128,128]{2,1,0:T(8,128)S(1)} fusion(f32[24,128,128]{2,1,0:T(8,128)S(1)} %fusion.10, f32[1,1,24,128,128]{4,3,2,1,0:T(8,128)S(1)} %bitcast_add_fusion), kind=kOutput, calls=%fused_computation.9 | convolution fusion | flops 603979776 | bytes 4718592 | tf_op jit(solution)/shard_map/glhrs,glhst->glhrt/dot_general | solution.py:50
  131.0 0.0 slice-start.3
  131.0 1.6 fusion.12
  132.6 1.7 %fusion.62 = f32[24,128,128]{2,1,0:T(8,128)S(1)} fusion(f32[24,128,128]{2,1,0:T(8,128)S(1)} %fusion.8), kind=kOutput, calls=%fused_computation.67 | convolution fusion | flops 603979776 | bytes 3145728 | tf_op jit(solution)/shard_map/glhrs,glhst->glhrt/dot_general | solution.py:45
  134.3 0.0 slice-start.4
  134.3 1.9 %fusion.25 = f32[24,128,128]{2,1,0:T(8,128)S(1)} fusion(f32[24,128,128]{2,1,0:T(8,128)S(1)} %fusion.8, f32[24,128,128]{2,1,0:T(8,128)S(1)} %fusion.62, f32[128,128]{1,0:T(8,128)S(1)} %fusion.48), kind=kOutput, calls=%fused_computation.28 | convolution fusion | flops 605552640 | bytes 4784128 | tf_op jit(solution)/shard_map/glhrs,glhst->glhrt/dot_general | solution.py:49
  136.2 0.0 slice-start
  136.2 2.1 %fusion.26 = f32[24,128,128]{2,1,0:T(8,128)S(1)} fusion(f32[24,128,128]{2,1,0:T(8,128)S(1)} %fusion.12, f32[24,128,128]{2,1,0:T(8,128)S(1)} %fusion.62, f32[24,128,128]{2,1,0:T(8,128)S(1)} %fusion.8, f32[128,128]{1,0:T(8,128)S(1)} %fusion.48), kind=kOutput, calls=%fused_computation.29 | convolution fusion | flops 605552640 | bytes 6356992 | tf_op jit(solution)/shard_map/glhrs,glhst->glhrt/dot_general | solution.py:47
  138.3 0.0 slice-start.1
  138.4 0.0 slice-start.5
  138.4 1.9 %fusion.24 = f32[24,128,128]{2,1,0:T(8,128)S(1)} fusion(f32[24,128,128]{2,1,0:T(8,128)S(1)} %fusion.25, f32[24,128,128]{2,1,0:T(8,128)S(1)} %fusion.62, f32[24,128,128]{2,1,0:T(8,128)S(1)} %fusion.8, f32[128,128]{1,0:T(8,128)S(1)} %fusion.48), kind=kOutput, calls=%fused_computation.27 | convolution fusion | flops 605552640 | bytes 6356992 | tf_op jit(solution)/shard_map/glhrs,glhst->glhrt/dot_general | solution.py:50
  140.2 0.0 slice-start.2
  140.3 1.7 %fusion.63 = f32[24,128,128]{2,1,0:T(8,128)S(1)} fusion(f32[24,128,128]{2,1,0:T(8,128)S(1)} %fusion.24), kind=kOutput, calls=%fused_computation.68 | convolution fusion | flops 603979776 | bytes 3145728 | tf_op jit(solution)/shard_map/glhrs,glhst->glhrt/dot_general | solution.py:45
  141.9 1.9 %fusion.19 = f32[24,128,128]{2,1,0:T(8,128)S(1)} fusion(f32[24,128,128]{2,1,0:T(8,128)S(1)} %fusion.26, f32[24,128,128]{2,1,0:T(8,128)S(1)} %fusion.63, f32[24,128,128]{2,1,0:T(8,128)S(1)} %fusion.24, f32[128,128]{1,0:T(8,128)S(1)} %fusion.48), kind=kOutput, calls=%fused_computation.21 | convolution fusion | flops 605552640 | bytes 6356992 | tf_op jit(solution)/shard_map/glhrs,glhst->glhrt/dot_general | solution.py:47
  143.8 0.0 slice-done.3
  143.8 0.0 slice-done.4
  143.8 0.0 slice-done
  143.8 0.0 slice-done.1
  143.8 0.0 slice-done.5
  143.9 0.0 slice-done.2
  143.9 11.6 %multiply_bitcast_fusion = f32[1,1,24,768,128]{4,3,2,1,0:T(8,128)} fusion(f32[24,128,128]{2,1,0:T(8,128)S(1)} %fusion.19, f32[24]{0:T(128)S(1)} %get-tuple-element.2, f32[1,1,24,768,128]{4,3,2,1,0:T(8,128)S(1)} %bitcast.49, f32[1,1,24,768,128]{4,3,2,1,0:T(8,128)S(1)} %bitcast.51), kind=kOutput, calls=%fused_computation.4 | convolution fusion | flops 3633315840 | bytes 29884512 | tf_op jit(solution)/shard_map/glhdr,glhrs->glhds/dot_general | solution.py:51
  (6 shorter events, 0.0 us)
Async XLA Ops:
  7.2 105.4 %all-reduce.2.cloned.1.call-start = ((), (), s32[]{:S(2)}) async-start(), calls=%async_computation | async-start | bytes 3145728 | tf_op jit(solution)/shard_map/psum | solution.py:22
  47.8 0.7 copy-start.1
  112.5 12.9 %copy-start = (f32[1,1,24,128,128]{4,3,2,1,0:T(8,128)S(1)}, f32[1,1,24,128,128]{4,3,2,1,0:T(8,128)}, u32[]{:S(2)}) copy-start(f32[1,1,24,128,128]{4,3,2,1,0:T(8,128)} %all-reduce.2.cloned.1.call-done) | copy-start | bytes 4718596
  131.0 12.8 %slice-start.3 = ((s8[9437184]{0:T(1024)(128)(4,1)}), s8[4194304]{0:T(1024)(128)(4,1)S(1)}, s32[]{:S(2)}) async-start(s8[9437184]{0:T(1024)(128)(4,1)} %bitcast.50), calls=%async_computation.4 | async-start | bytes 8388608
  134.3 9.5 %slice-start.4 = ((s8[9437184]{0:T(1024)(128)(4,1)}), s8[4194304]{0:T(1024)(128)(4,1)S(1)}, s32[]{:S(2)}) async-start(s8[9437184]{0:T(1024)(128)(4,1)} %bitcast.50), calls=%async_computation.5 | async-start | bytes 8388608
  136.2 7.6 %slice-start = ((s8[9437184]{0:T(1024)(128)(4,1)}), s8[4194304]{0:T(1024)(128)(4,1)S(1)}, s32[]{:S(2)}) async-start(s8[9437184]{0:T(1024)(128)(4,1)} %bitcast.48), calls=%async_computation.1 | async-start | bytes 8388608
  138.3 5.5 %slice-start.1 = ((s8[9437184]{0:T(1024)(128)(4,1)}), s8[4194304]{0:T(1024)(128)(4,1)S(1)}, s32[]{:S(2)}) async-start(s8[9437184]{0:T(1024)(128)(4,1)} %bitcast.48), calls=%async_computation.2 | async-start | bytes 8388608
  138.4 5.5 %slice-start.5 = ((s8[9437184]{0:T(1024)(128)(4,1)}), s8[1048576]{0:T(1024)(128)(4,1)S(1)}, s32[]{:S(2)}) async-start(s8[9437184]{0:T(1024)(128)(4,1)} %bitcast.50), calls=%async_computation.6 | async-start | bytes 2097152
  140.2 3.6 %slice-start.2 = ((s8[9437184]{0:T(1024)(128)(4,1)}), s8[1048576]{0:T(1024)(128)(4,1)S(1)}, s32[]{:S(2)}) async-start(s8[9437184]{0:T(1024)(128)(4,1)} %bitcast.48), calls=%async_computation.3 | async-start | bytes 2097152
Sparse Core Ops, SparseCore 0:
  47.9 64.5 all-reduce.1
where the time goes:
time: 162 us
  waiting for transfers between devices  62.7 us (39%)
  matrix products  61.7 us (38%)
  between operations  14.9 us (9%)
  other arithmetic  12.4 us (8%)
  blocking collectives  9.78 us (6%)
    psum x1, waiting for transfers between devices, summed_gram(): return lax.psum(partial_gram, 'col')  62.7 us
    dot_general x1, matrix products, summed_gram(): jnp.einsum('glhdr,glhds->glhrs', stack, stack, precision=PRECISE)  29 us
    add x1, other arithmetic, on_device(): new_momentum = MOMENTUM_DECAY * momentum + gradient  11.6 us
    dot_general x1, matrix products, on_device(): jnp.einsum('glhdr,glhrs->glhds', scaled, total, precision=PRECISE)  11.6 us
    pmax x1, blocking collectives, head_bound(): overall = lax.pmax(local_most, ('grp', 'lay'))  9.78 us
    dot_general x3, matrix products, on_device(): total = jnp.einsum('glhrs,glhst->glhrt', total, mixing, precision=PRECISE)  5.55 us
    dot_general x3, matrix products, on_device(): jnp.einsum('glhrs,glhst->glhrt', current, current, precision=PRECISE)  5.4 us
    dot_general x2, matrix products, on_device(): jnp.einsum('glhrs,glhst->glhrt', mixing, current, precision=PRECISE)  3.67 us
  transfers between devices with their start and end apart: 1, of which 1 were waited for; matrix products, arithmetic and copies ran while one was open for 0% of the time, Pallas kernels for 0%

commit v1 on v0

--- a/solution.py
+++ b/solution.py
@@ -1,11 +1,14 @@
+import functools
 import math
 
 import jax
 import jax.numpy as jnp
 from jax import lax
+from jax.experimental import pallas as pl
+from jax.experimental.pallas import tpu as pltpu
 from jax.sharding import PartitionSpec as P
 
-D = 6144
+
 ITERS = 3
 
 
@@ -29,7 +32,7 @@
     return 2.0 * jnp.sqrt(overall)
 
 
-def on_device(gradient, momentum, probe_vector):
+def on_device_general(gradient, momentum, probe_vector):
     new_momentum = MOMENTUM_DECAY * momentum + gradient
     blend = gradient + MOMENTUM_DECAY * new_momentum
     width = blend.shape[-1]
@@ -49,13 +52,357 @@
             halfway = jnp.einsum("glhrs,glhst->glhrt", mixing, current, precision=PRECISE)
             current = jnp.einsum("glhrs,glhst->glhrt", halfway, mixing, precision=PRECISE)
     polished = jnp.einsum("glhdr,glhrs->glhds", scaled, total, precision=PRECISE)
-    update = polished * (0.2 * math.sqrt(D))
+    update = polished * (0.2 * math.sqrt(blend.shape[3] * lax.psum(1, "col")))
     return (new_momentum, update)
 
 
+F32 = jnp.float32
+BF16 = jnp.bfloat16
+VMEM_LIMIT = 60 * 2**20
+ROOMY = 48 * 2**20
+
+
+def iotas(shape):
+    return lax.broadcasted_iota(jnp.int32, shape, 0), lax.broadcasted_iota(jnp.int32, shape, 1)
+
+
+def packed_rows(heads, width):
+    full, odd = divmod(heads, 2)
+    return full * width + odd * (width // 2) + 8 * (full + odd)
+
+
+def pack(mats):
+    width = mats[0].shape[0]
+    row, col = iotas((width, width))
+    rows8, _ = iotas((8, width))
+    body, diags = [], []
+    for i in range(0, len(mats) - 1, 2):
+        first, second = mats[i], mats[i + 1]
+        body.append(jnp.where(row >= col, first, second))
+        diag = jnp.sum(jnp.where(row == col, second, 0.0), axis=0, keepdims=True)
+        diags.append(jnp.where(rows8 == 0, diag, 0.0))
+    if len(mats) % 2:
+        half = width // 2
+        last = mats[-1]
+        row, col = iotas((half, width))
+        rolled = pltpu.roll(last[half:], half, 1)
+        body.append(jnp.where((col < half) & (col > row), rolled, last[:half]))
+        diag = jnp.sum(jnp.where(row == col, rolled, 0.0), axis=0, keepdims=True)
+        diags.append(jnp.where(rows8 == 0, diag, 0.0))
+    return body + diags
+
+
+def store_packed(ref, mats):
+    start = 0
+    for piece in pack(mats):
+        ref[start : start + piece.shape[0]] = piece
+        start += piece.shape[0]
+
+
+def unpack(value, heads):
+    width = value.shape[1]
+    half = width // 2
+    full, odd = divmod(heads, 2)
+    diag_start = full * width + odd * half
+    row, col = iotas((width, width))
+    mats = []
+    for i in range(full):
+        square = value[i * width : (i + 1) * width]
+        turned = square.T
+        diag = value[diag_start + 8 * i : diag_start + 8 * i + 1]
+        mats.append(jnp.where(row >= col, square, turned))
+        mats.append(jnp.where(row < col, square, jnp.where(row > col, turned, diag)))
+    if odd:
+        top = value[full * width : full * width + half]
+        turned = jnp.concatenate([top, jnp.zeros_like(top)], axis=0).T
+        diag = value[diag_start + 8 * full : diag_start + 8 * full + 1]
+        row, col = iotas((half, width))
+        upper = jnp.where((col < half) & (row < col), turned[:half], top)
+        corner = jnp.where(row < col, top, jnp.where(row > col, turned[:half], diag))
+        lower = jnp.where(col < half, turned[half:], pltpu.roll(corner, half, 1))
+        mats.append(jnp.concatenate([upper, lower], axis=0))
+    return mats
+
+
+def split(value):
+    high = value.astype(BF16)
+    return high, (value - high.astype(F32)).astype(BF16)
+
+
+def head_specs(per, shape):
+    return [pl.BlockSpec((1,) + shape, lambda j, ids, i=i: (ids[j] * per + i, 0, 0)) for i in range(per)]
+
+
+def gram_kernel(per, group_ref, *refs):
+    del group_ref
+    gradient_refs, momentum_refs, refs = refs[:per], refs[per : 2 * per], refs[2 * per :]
+    mats = []
+    for gradient_ref, momentum_ref in zip(gradient_refs, momentum_refs):
+        gradient = gradient_ref[0]
+        blend = gradient + MOMENTUM_DECAY * (MOMENTUM_DECAY * momentum_ref[0] + gradient)
+        high, low = split(blend)
+        both = jnp.concatenate([high, low], axis=1)
+        product = lax.dot_general(high, both, (((0,), (0,)), ((), ())), preferred_element_type=F32)
+        width = blend.shape[1]
+        cross = product[:, width:]
+        mats.append(product[:, :width] + (cross + cross.T))
+    if len(refs) == 1:
+        store_packed(refs[0].at[0], mats)
+        return
+    other_ref, *out_refs, held_ref = refs
+    store_packed(held_ref, mats)
+    for k, out_ref in enumerate(out_refs):
+
+        @pl.when(pl.program_id(0) == k)
+        def _(out_ref=out_ref):
+            out_ref[...] = held_ref[...] + other_ref[0]
+
+
+def local_grams(groups, gradient, momentum, per, other=None):
+    _, rows, width = gradient.shape
+    count = groups.shape[0]
+    blocks = head_specs(per, (rows, width))
+    packed = packed_rows(per, width)
+    piece = pl.BlockSpec((1, packed, width), lambda j, ids: (j, 0, 0))
+    operands, in_specs = [groups] + [gradient] * per + [momentum] * per, blocks + blocks
+    if other is None:
+        out_shape = jax.ShapeDtypeStruct((count, packed, width), F32)
+        out_specs, scratch = piece, []
+    else:
+        operands.append(other)
+        in_specs.append(piece)
+        out_shape = [jax.ShapeDtypeStruct((packed, width), F32)] * count
+        out_specs = [pl.BlockSpec((packed, width), lambda j, ids: (0, 0))] * count
+        scratch = [pltpu.VMEM((packed, width), F32)]
+    return pl.pallas_call(
+        functools.partial(gram_kernel, per),
+        name="local_grams",
+        out_shape=out_shape,
+        grid_spec=pltpu.PrefetchScalarGridSpec(
+            num_scalar_prefetch=1,
+            grid=(count,),
+            in_specs=in_specs,
+            out_specs=out_specs,
+            scratch_shapes=scratch,
+        ),
+        cost_estimate=pl.CostEstimate(
+            flops=count * per * rows * width * width * 8,
+            bytes_accessed=count * per * rows * width * 8,
+            transcendentals=0,
+        ),
+        compiler_params=pltpu.CompilerParams(vmem_limit_bytes=VMEM_LIMIT),
+    )(*operands)
+
+
+def momentum_kernel(per, *refs):
+    new_ref, halves_ref = refs[-2:]
+    for i in range(per):
+        gradient = refs[i][0]
+        new = MOMENTUM_DECAY * refs[per + i][0] + gradient
+        new_ref[i] = new
+        high, low = split(gradient + MOMENTUM_DECAY * new)
+        width = gradient.shape[1]
+        halves_ref[i, :, :width] = high
+        halves_ref[i, :, width:] = low
+
+
+def update_momentum(gradient, momentum, per, start, stop, partly=()):
+    heads, rows, width = gradient.shape
+    by_group = lambda j: (j + start, 0, 0)
+    block = pl.BlockSpec((per, rows, width), by_group)
+    heads_of = [pl.BlockSpec((1, rows, width), lambda j, i=i: ((j + start) * per + i, 0, 0)) for i in range(per)]
+    return pl.pallas_call(
+        functools.partial(momentum_kernel, per),
+        name="update_momentum",
+        grid=(stop - start,),
+        in_specs=heads_of + heads_of + [pl.BlockSpec(memory_space=pl.ANY)] * len(partly),
+        out_specs=[block, pl.BlockSpec((per, rows, 2 * width), by_group)],
+        out_shape=[
+            jax.ShapeDtypeStruct(gradient.shape, F32),
+            jax.ShapeDtypeStruct((heads, rows, 2 * width), BF16),
+        ],
+        input_output_aliases={2 * per: 0, 2 * per + 1: 1} if partly else {},
+        cost_estimate=pl.CostEstimate(
+            flops=(stop - start) * per * rows * width * 400,
+            bytes_accessed=(stop - start) * per * rows * width * 16,
+            transcendentals=0,
+        ),
+        compiler_params=pltpu.CompilerParams(vmem_limit_bytes=ROOMY),
+    )(*[gradient] * per, *[momentum] * per, *partly)
+
+
+def estimate_kernel(per, probe_ref, *refs):
+    *pieces, gram_ref, estimate_ref = refs
+    total = pieces[0][...]
+    for piece in pieces[1:]:
+        total = total + piece[...]
+    probe = probe_ref[...]
+    probe_norm = jnp.sqrt(jnp.sum(probe * probe, keepdims=True) + EPSILON)
+    row, _ = iotas(estimate_ref.shape)
+    estimates = jnp.zeros(estimate_ref.shape, F32)
+    for i, gram in enumerate(unpack(total, per)):
+        gram_ref[i] = gram
+        product = jnp.sum(gram * probe, axis=1, keepdims=True)
+        estimate = jnp.sqrt(jnp.sum(product * product, keepdims=True) + EPSILON) / probe_norm
+        estimates = jnp.where(row == i, estimate, estimates)
+    estimate_ref[...] = estimates
+
+
+def sum_and_estimate(pieces, probe, per):
+    width = pieces[0].shape[1]
+    return pl.pallas_call(
+        functools.partial(estimate_kernel, per),
+        name="sum_and_estimate",
+        out_shape=[
+            jax.ShapeDtypeStruct((per, width, width), F32),
+            jax.ShapeDtypeStruct((-(-per // 8) * 8, width), F32),
+        ],
+    )(probe, *pieces)
+
+
+def precise_dot(left, right):
+    return jnp.dot(left, right, precision=PRECISE, preferred_element_type=F32)
+
+
+def newton_schulz_kernel(depth, estimate_ref, gram_ref, out_ref):
+    per, width = gram_ref.shape[:2]
+    row, col = iotas((width, width))
+    identity = jnp.where(row == col, 1.0, 0.0)
+    bounds = [2.0 * jnp.sqrt(estimate_ref[i : i + 1]) for i in range(per)]
+    current = [gram_ref[i] / (bounds[i] * bounds[i]) for i in range(per)]
+    total = None
+    for counter in range(ITERS):
+        square = [precise_dot(a, a) for a in current]
+        mixing = [
+            LINEAR_TERM * identity + CUBIC_TERM * a + QUINTIC_TERM * s for a, s in zip(current, square)
+        ]
+        if counter + 1 < ITERS:
+            halfway = [precise_dot(m, a) for m, a in zip(mixing, current)]
+            current = [precise_dot(h, m) for h, m in zip(halfway, mixing)]
+        total = mixing if total is None else [precise_dot(t, m) for t, m in zip(total, mixing)]
+    scale = 0.2 * math.sqrt(depth)
+    store_packed(out_ref, [t * (scale / b) for t, b in zip(total, bounds)])
+
+
+def newton_schulz(estimate, gram, depth):
+    per, width = gram.shape[:2]
+    return pl.pallas_call(
+        functools.partial(newton_schulz_kernel, depth),
+        name="newton_schulz",
+        out_shape=jax.ShapeDtypeStruct((packed_rows(per, width), width), F32),
+    )(estimate, gram)
+
+
+def apply_kernel(group_ref, factor_ref, *refs):
+    del group_ref
+    out_ref = refs[-1]
+    per, _, width = out_ref.shape
+    for i, factor in enumerate(unpack(factor_ref[0], per)):
+        high, low = split(factor)
+        right = jnp.concatenate(
+            [
+                jnp.concatenate([high, low], axis=1),
+                jnp.concatenate([high, jnp.zeros_like(low)], axis=1),
+            ],
+            axis=0,
+        )
+        product = jnp.dot(refs[i][0], right, preferred_element_type=F32)
+        out_ref[i] = product[:, :width] + product[:, width:]
+
+
+def apply_factors(groups, factors, halves, per, partly=None):
+    heads, rows, double = halves.shape
+    width = double // 2
+    count, packed = factors.shape[:2]
+    by_group = lambda j, ids: (ids[j], 0, 0)
+    operands = [groups, factors] + [halves] * per
+    in_specs = [
+        pl.BlockSpec((1, packed, width), lambda j, ids: (j, 0, 0)),
+        *head_specs(per, (rows, double)),
+    ]
+    aliases = {}
+    if partly is not None:
+        operands.append(partly)
+        in_specs.append(pl.BlockSpec(memory_space=pl.ANY))
+        aliases = {2 + per: 0}
+    return pl.pallas_call(
+        apply_kernel,
+        name="apply_factors",
+        out_shape=jax.ShapeDtypeStruct((heads, rows, width), F32),
+        grid_spec=pltpu.PrefetchScalarGridSpec(
+            num_scalar_prefetch=1,
+            grid=(count,),
+            in_specs=in_specs,
+            out_specs=pl.BlockSpec((per, rows, width), by_group),
+        ),
+        input_output_aliases=aliases,
+        cost_estimate=pl.CostEstimate(
+            flops=count * per * rows * width * width * 8,
+            bytes_accessed=count * per * rows * width * 8,
+            transcendentals=0,
+        ),
+        compiler_params=pltpu.CompilerParams(vmem_limit_bytes=ROOMY),
+    )(*operands)
+
+
+def swap(value, distance, devices):
+    return lax.ppermute(value, "col", [(i, i ^ distance) for i in range(devices)])
+
+
+def on_device(gradient, momentum, probe_vector, devices, axis_sizes):
+    shape = gradient.shape
+    heads, rows, width = shape[2:]
+    gradient = gradient.reshape(heads, rows, width)
+    momentum = momentum.reshape(heads, rows, width)
+    chips = devices // 2
+    per = heads // devices
+    place = lax.axis_index("col")
+    mine = jnp.stack([place ^ (2 * k) for k in range(chips)]).astype(jnp.int32)
+    theirs = mine ^ 1
+    groups = heads // per
+    early = groups - groups // 3
+    for_sibling = local_grams(theirs, gradient, momentum, per)
+    from_sibling = swap(for_sibling, 1, devices)
+    sums = local_grams(mine, gradient, momentum, per, from_sibling)
+    pieces = [sums[0]]
+    for k in range(1, chips):
+        pieces.append(swap(sums[k], 2 * k, devices))
+    gradient, momentum, anchor = lax.optimization_barrier((gradient, momentum, sums[0]))
+    pieces[0] = anchor
+    partly = update_momentum(gradient, momentum, per, 0, early)
+    gram, estimate = sum_and_estimate(pieces, probe_vector.reshape(1, width), per)
+    for name, size in axis_sizes:
+        others = [
+            lax.ppermute(estimate, name, [(i, (i + k) % size) for i in range(size)]) for k in range(1, size)
+        ]
+        for other in others:
+            estimate = jnp.maximum(estimate, other)
+    factor = newton_schulz(estimate, gram, rows * devices)
+    factors = [factor]
+    for k in range(1, chips):
+        factors.append(swap(factor, 2 * k, devices))
+    gradient, momentum, *partly = lax.optimization_barrier((gradient, momentum, *partly))
+    new_momentum, halves = update_momentum(gradient, momentum, per, early, groups, partly)
+    factors = jnp.stack(factors)
+    sibling_factors = swap(factors, 1, devices)
+    update = apply_factors(mine, factors, halves, per)
+    update = apply_factors(theirs, sibling_factors, halves, per, update)
+    return new_momentum.reshape(shape), update.reshape(shape)
+
+
 def solution(mesh):
+    sizes = dict(mesh.shape)
+    devices = sizes["col"]
+    axis_sizes = (("grp", sizes["grp"]), ("lay", sizes["lay"]))
+
+    def body(gradient, momentum, probe_vector):
+        groups, layers, heads = gradient.shape[:3]
+        if groups == 1 and layers == 1 and heads % devices == 0 and devices > 1 and devices & (devices - 1) == 0:
+            return on_device(gradient, momentum, probe_vector, devices, axis_sizes)
+        return on_device_general(gradient, momentum, probe_vector)
+
     in_specs = (P("grp", "lay", None, "col", None), P("grp", "lay", None, "col", None), P())
     out_specs = (P("grp", "lay", None, "col", None), P("grp", "lay", None, "col", None))
     return jax.shard_map(
-        on_device, mesh=mesh, in_specs=in_specs, out_specs=out_specs, check_vma=False
+        body, mesh=mesh, in_specs=in_specs, out_specs=out_specs, check_vma=False
     )

time: 162 us -> 88 us (0.54)
  matrix products: 61.7 us -> 0 us
  Pallas kernels: 0 us -> 48.3 us
  waiting for transfers between devices: 62.7 us -> 20.7 us
  between operations: 14.9 us -> 0.68 us
  starting transfers between devices: 0.04 us -> 13.4 us
  blocking collectives: 9.78 us -> 0 us
  other arithmetic: 12.4 us -> 2.82 us
    psum x1 -> x0, waiting for transfers between devices: 62.7 us -> none  [summed_gram(): return lax.psum(partial_gram, 'col')]
    dot_general x13 -> x0, matrix products: 61.7 us -> none  [the longest x1 29 us: summed_gram(): jnp.einsum('glhdr,glhds->glhrs', stack, stack, precision=PRECISE)]
    pallas_call x0 -> x8, Pallas kernels: none -> 48.3 us  [the longest x2 15.8 us: update_momentum(): pl.pallas_call(functools.partial(momentum_kernel, per), name='update_mome...]
    ppermute x0 -> x10, waiting for transfers between devices: none -> 20.7 us  [the longest x8 16.5 us: swap(): lax.ppermute(value, 'col', [(i, i ^ distance) for i in range(devices)])]
    ppermute x0 -> x10, starting transfers between devices: none -> 13.4 us  [the longest x8 10.3 us: swap(): lax.ppermute(value, 'col', [(i, i ^ distance) for i in range(devices)])]
    add x1 -> x0, other arithmetic: 11.6 us -> none  [on_device(): new_momentum = MOMENTUM_DECAY * momentum + gradient]
    pmax x1 -> x0, blocking collectives: 9.78 us -> none  [head_bound(): overall = lax.pmax(local_most, ('grp', 'lay'))]
  transfers between devices with their start and end apart: 1 -> 10, of which waited for: 1 -> 8; matrix products, arithmetic and copies ran while one was open for 0% -> 0% of each run, Pallas kernels for 0% -> 26%
where the time goes in v1:
time: 88 us; the launch traced here: 87.4 us
  Pallas kernels  48.3 us (55%)
  waiting for transfers between devices  20.7 us (24%)
  starting transfers between devices  13.4 us (15%)
  other arithmetic  2.82 us (3%)
  local copies, waits for them, and re-layouts  1.44 us (2%)
    ppermute x8, waiting for transfers between devices, swap(): lax.ppermute(value, 'col', [(i, i ^ distance) for i in range(devices)])  16.5 us
    pallas_call x2, Pallas kernels, update_momentum(): pl.pallas_call(functools.partial(momentum_kernel, per), name='update_mome...  15.8 us
    pallas_call x2, Pallas kernels, local_grams(): pl.pallas_call(functools.partial(gram_kernel, per), name='local_grams', o...  13.6 us
    pallas_call x2, Pallas kernels, apply_factors(): pl.pallas_call(apply_kernel, name='apply_factors', out_shape=jax.ShapeDty...  13.3 us
    ppermute x8, starting transfers between devices, swap(): lax.ppermute(value, 'col', [(i, i ^ distance) for i in range(devices)])  10.3 us
    ppermute x2, waiting for transfers between devices, on_device(): lax.ppermute(estimate, name, [(i, (i + k) % size) for i in range(size)])  4.29 us
    pallas_call x1, Pallas kernels, newton_schulz(): pl.pallas_call(functools.partial(newton_schulz_kernel, depth), name='newt...  3.63 us
    ppermute x2, starting transfers between devices, on_device(): lax.ppermute(estimate, name, [(i, (i + k) % size) for i in range(size)])  3.13 us
  transfers between devices with their start and end apart: 10, of which 8 were waited for; matrix products, arithmetic and copies ran while one was open for 0% of the time, Pallas kernels for 26%

profile of v1, /device:TPU:0, one launch (start us, length us, event | category | flops | bytes accessed | tf_op | source)
XLA Modules:
  0.0 87.4 jit_solution(1570588294031937824)
XLA Ops:
  0.6 0.6 broadcast_xor_fusion
  1.3 6.7 %local_grams.2 = f32[4,208,128]{2,1,0:T(8,128)} custom-call(s32[4]{0:T(128)} %get-tuple-element.36.group_ref, f32[24,768,128]{2,1,0:T(8,128)} %bitcast.13, f32[24,768,128]{2,1,0:T(8,128)} %bitcast.14, f32[24,768,128]{2,1,0:T(8,128)} %bitcast.15, f32[24,768,128]{2,1,0:T(8,128)} %bitcast.25, f32[24,768,128]{2,1,0:T(8,128)} %bitcast.26, f32[24,768,128]{2,1,0:T(8,128)} %bitcast.27), custom_call_target="tpu_custom_call" | custom-call | flops 1207959552 | bytes 9437184 | tf_op jit(solution)/shard_map/local_grams/pallas_call | solution.py:177
  7.9 0.5 collective-permute-start
  8.4 1.6 %collective-permute-done.refs_6_ = f32[4,208,128]{2,1,0:T(8,128)S(1)} collective-permute-done((f32[4,208,128]{2,1,0:T(8,128)}, f32[4,208,128]{2,1,0:T(8,128)S(1)}, u32[]{:S(2)}, u32[]{:S(2)}) %collective-permute-start) | collective-permute-done | bytes 426016 | tf_op jit(solution)/shard_map/ppermute | solution.py:349
  10.0 0.0 copy-start.2
  10.0 0.8 copy-done.2
  10.8 6.9 %local_grams.3 = (f32[208,128]{1,0:T(8,128)}, f32[208,128]{1,0:T(8,128)}, f32[208,128]{1,0:T(8,128)}, f32[208,128]{1,0:T(8,128)}) custom-call(s32[4]{0:T(128)} %get-tuple-element.37.group_ref, f32[24,768,128]{2,1,0:T(8,128)} %bitcast.16, f32[24,768,128]{2,1,0:T(8,128)} %bitcast.17, f32[24,768,128]{2,1,0:T(8,128)} %bitcast.18, f32[24,768,128]{2,1,0:T(8,128)} %bitcast.28, ...), custom_call_target="tpu_custom_call" | custom-call | flops 1207959552 | bytes 9437184 | tf_op jit(solution)/shard_map/local_grams/pallas_call | solution.py:177
  17.7 2.9 %collective-permute-start.1 = (f32[208,128]{1,0:T(8,128)}, f32[208,128]{1,0:T(8,128)S(1)}, u32[]{:S(2)}, u32[]{:S(2)}) collective-permute-start(f32[208,128]{1,0:T(8,128)} %get-tuple-element.30), channel_id=1, source_target_pairs={{0,4},{2,6},{4,0},{6,2},{8,12},{10,14},{12,8},{14,10},{1,5},{3,7},... | collective-permute-start | bytes 319496 | tf_op jit(solution)/shard_map/ppermute | solution.py:349
  20.6 2.6 %collective-permute-start.2 = (f32[208,128]{1,0:T(8,128)}, f32[208,128]{1,0:T(8,128)S(1)}, u32[]{:S(2)}, u32[]{:S(2)}) collective-permute-start(f32[208,128]{1,0:T(8,128)} %get-tuple-element.31), channel_id=1, source_target_pairs={{0,8},{2,10},{4,12},{6,14},{8,0},{10,2},{12,4},{14,6},{1,9},{3,11}... | collective-permute-start | bytes 319496 | tf_op jit(solution)/shard_map/ppermute | solution.py:349
  23.2 0.0 collective-permute-start.3
  23.2 0.9 collective-permute-done.1.refs_1_
  24.1 0.0 copy-start.3
  24.1 7.9 %collective-permute-done.2.refs_2_ = f32[208,128]{1,0:T(8,128)S(1)} collective-permute-done((f32[208,128]{1,0:T(8,128)}, f32[208,128]{1,0:T(8,128)S(1)}, u32[]{:S(2)}, u32[]{:S(2)}) %collective-permute-start.2) | collective-permute-done | bytes 106528 | tf_op jit(solution)/shard_map/ppermute | solution.py:349
  32.0 0.0 copy-start.4
  32.0 0.0 collective-permute-done.3.refs_3_
  32.0 0.0 copy-start.5
  32.0 0.0 copy-done.3
  32.0 0.6 copy-done.4
  32.7 0.0 copy-done.5
  32.7 2.0 %sum_and_estimate.1 = (f32[3,128,128]{2,1,0:T(8,128)}, f32[8,128]{1,0:T(8,128)}) custom-call(f32[1,128]{1,0:T(1,128)} %bitcast.43, f32[208,128]{1,0:T(8,128)} %get-tuple-element.29.refs_0_, f32[208,128]{1,0:T(8,128)} %copy-done.3, f32[208,128]{1,0:T(8,128)} %copy-done.4, f32[208,128]{1,0:T(8,128)} %copy-done.5), custom_call_target="tpu_custom_call" | custom-call | tf_op jit(solution)/shard_map/sum_and_estimate/pallas_call | solution.py:253
  34.7 1.6 %collective-permute-start.4 = (f32[8,128]{1,0:T(8,128)}, f32[8,128]{1,0:T(8,128)S(1)}, u32[]{:S(2)}, u32[]{:S(2)}) collective-permute-start(f32[8,128]{1,0:T(8,128)} %get-tuple-element.33), channel_id=1, source_target_pairs={{0,16},{16,0},{1,17},{17,1},{2,18},{18,2},{3,19},{19,3},{4,20},{20... | collective-permute-start | bytes 12296 | tf_op jit(solution)/shard_map/ppermute | solution.py:376
  36.3 2.3 %collective-permute-done.4 = f32[8,128]{1,0:T(8,128)S(1)} collective-permute-done((f32[8,128]{1,0:T(8,128)}, f32[8,128]{1,0:T(8,128)S(1)}, u32[]{:S(2)}, u32[]{:S(2)}) %collective-permute-start.4) | collective-permute-done | bytes 4128 | tf_op jit(solution)/shard_map/ppermute | solution.py:376
  38.5 0.7 max.6
  39.2 1.6 %collective-permute-start.5 = (f32[8,128]{1,0:T(8,128)S(1)}, f32[8,128]{1,0:T(8,128)S(1)}, u32[]{:S(2)}, u32[]{:S(2)}) collective-permute-start(f32[8,128]{1,0:T(8,128)S(1)} %max.6), channel_id=1, source_target_pairs={{0,1},{1,0},{2,3},{3,2},{4,5},{5,4},{6,7},{7,6},{8,9},{9,8},{10,11... | collective-permute-start | bytes 12296 | tf_op jit(solution)/shard_map/ppermute | solution.py:376
  40.8 2.0 %collective-permute-done.5 = f32[8,128]{1,0:T(8,128)S(1)} collective-permute-done((f32[8,128]{1,0:T(8,128)S(1)}, f32[8,128]{1,0:T(8,128)S(1)}, u32[]{:S(2)}, u32[]{:S(2)}) %collective-permute-start.5) | collective-permute-done | bytes 4128 | tf_op jit(solution)/shard_map/ppermute | solution.py:376
  42.8 0.6 max.7.estimate_ref
  43.4 3.6 %newton_schulz.1 = f32[208,128]{1,0:T(8,128)} custom-call(f32[8,128]{1,0:T(8,128)} %max.7.estimate_ref, f32[3,128,128]{2,1,0:T(8,128)} %get-tuple-element.34.gram_ref), custom_call_target="tpu_custom_call" | custom-call | tf_op jit(solution)/shard_map/newton_schulz/pallas_call | solution.py:289
  47.0 2.9 %collective-permute-start.7 = (f32[208,128]{1,0:T(8,128)}, f32[208,128]{1,0:T(8,128)S(1)}, u32[]{:S(2)}, u32[]{:S(2)}) collective-permute-start(f32[208,128]{1,0:T(8,128)} %newton_schulz.1), channel_id=1, source_target_pairs={{0,8},{2,10},{4,12},{6,14},{8,0},{10,2},{12,4},{14,6},{1,9},{3,11}... | collective-permute-start | bytes 319496 | tf_op jit(solution)/shard_map/ppermute | solution.py:349
  49.9 1.3 %collective-permute-start.8 = (f32[208,128]{1,0:T(8,128)}, f32[208,128]{1,0:T(8,128)S(1)}, u32[]{:S(2)}, u32[]{:S(2)}) collective-permute-start(f32[208,128]{1,0:T(8,128)} %newton_schulz.1), channel_id=1, source_target_pairs={{0,12},{2,14},{4,8},{6,10},{8,4},{10,6},{12,0},{14,2},{1,13},{3,15... | collective-permute-start | bytes 319496 | tf_op jit(solution)/shard_map/ppermute | solution.py:349
  51.2 0.0 collective-permute-start.6
  51.2 3.3 %collective-permute-done.7 = f32[208,128]{1,0:T(8,128)S(1)} collective-permute-done((f32[208,128]{1,0:T(8,128)}, f32[208,128]{1,0:T(8,128)S(1)}, u32[]{:S(2)}, u32[]{:S(2)}) %collective-permute-start.7) | collective-permute-done | bytes 106528 | tf_op jit(solution)/shard_map/ppermute | solution.py:349
  54.5 2.2 %collective-permute-done.8 = f32[208,128]{1,0:T(8,128)S(1)} collective-permute-done((f32[208,128]{1,0:T(8,128)}, f32[208,128]{1,0:T(8,128)S(1)}, u32[]{:S(2)}, u32[]{:S(2)}) %collective-permute-start.8) | collective-permute-done | bytes 106528 | tf_op jit(solution)/shard_map/ppermute | solution.py:349
  56.7 0.5 collective-permute-done.6
  57.3 0.9 %pad_maximum_fusion.factor_ref = f32[4,208,128]{2,1,0:T(8,128)S(1)} fusion(f32[1,208,128]{2,1,0:T(8,128)S(1)} %bitcast.41, f32[1,208,128]{2,1,0:T(8,128)S(1)} %bitcast.40, f32[1,208,128]{2,1,0:T(8,128)S(1)} %bitcast.42, f32[1,208,128]{2,1,0:T(8,128)} %bitcast.39), kind=kLoop, calls=%fused_computation | loop fusion | flops 319488 | bytes 851968 | tf_op jit(solution)/shard_map/stack | solution.py:386
  58.2 0.1 collective-permute-start.9
  58.3 11.6 %update_momentum.2 = (f32[24,768,128]{2,1,0:T(8,128)}, bf16[24,768,256]{2,1,0:T(8,128)(2,1)}) custom-call(f32[24,768,128]{2,1,0:T(8,128)} %bitcast.19, f32[24,768,128]{2,1,0:T(8,128)} %bitcast.20, f32[24,768,128]{2,1,0:T(8,128)} %bitcast.21, f32[24,768,128]{2,1,0:T(8,128)} %bitcast.31, f32[24,768,128]{2,1,0:T(8,128)} %bitcast.32, f32[24,768,128]{2,1,0:T(8,128)} %bitcast.33), custom_call_target="tpu_custom_call" | custom-call | flops 707788800 | bytes 28311552 | tf_op jit(solution)/shard_map/update_momentum/pallas_call | solution.py:214
  69.8 0.0 copy-start
  69.8 4.2 %update_momentum.3 = (f32[24,768,128]{2,1,0:T(8,128)}, bf16[24,768,256]{2,1,0:T(8,128)(2,1)}) custom-call(f32[24,768,128]{2,1,0:T(8,128)} %bitcast.22, f32[24,768,128]{2,1,0:T(8,128)} %bitcast.23, f32[24,768,128]{2,1,0:T(8,128)} %bitcast.24, f32[24,768,128]{2,1,0:T(8,128)} %bitcast.34, ...), custom_call_target="tpu_custom_call", output_to_operand_aliasing={{0}: (6, {}), {1}: (7, {})} | custom-call | flops 235929600 | bytes 9437184 | tf_op jit(solution)/shard_map/update_momentum/pallas_call | solution.py:214
  74.1 0.0 copy-done
  74.1 0.0 copy-start.1
  74.1 6.7 %apply_factors.2.refs_3_ = f32[24,768,128]{2,1,0:T(8,128)} custom-call(s32[4]{0:T(128)S(1)} %copy-done, f32[4,208,128]{2,1,0:T(8,128)S(1)} %pad_maximum_fusion.factor_ref, bf16[24,768,256]{2,1,0:T(8,128)(2,1)} %get-tuple-element.35.refs_0_.refs_1_.refs_2_, bf16[24,768,256]{2,1,0:T(8,128)(2,1)} %get-tuple-element.35.refs_0_.refs_1_.refs_2_, ...), custom_call_target="tpu_custom_call" | custom-call | flops 1207959552 | bytes 9437184 | tf_op jit(solution)/shard_map/apply_factors/pallas_call | solution.py:328
  80.8 0.0 collective-permute-done.9.factor_ref
  80.8 0.0 copy-done.1
  80.8 6.7 %apply_factors.3 = f32[24,768,128]{2,1,0:T(8,128)} custom-call(s32[4]{0:T(128)S(1)} %copy-done.1, f32[4,208,128]{2,1,0:T(8,128)S(1)} %collective-permute-done.9.factor_ref, bf16[24,768,256]{2,1,0:T(8,128)(2,1)} %get-tuple-element.35.refs_0_.refs_1_.refs_2_, ...), custom_call_target="tpu_custom_call", output_to_operand_aliasing={{}: (5, {})} | custom-call | flops 1207959552 | bytes 9437184 | tf_op jit(solution)/shard_map/apply_factors/pallas_call | solution.py:328
Async XLA Ops:
  7.9 2.1 %collective-permute-start = (f32[4,208,128]{2,1,0:T(8,128)}, f32[4,208,128]{2,1,0:T(8,128)S(1)}, u32[]{:S(2)}, u32[]{:S(2)}) collective-permute-start(f32[4,208,128]{2,1,0:T(8,128)} %local_grams.2), channel_id=1, source_target_pairs={{0,2},{2,0},{4,6},{6,4},{8,10},{10,8},{12,14},{14,12},{1,3},{3,1},... | collective-permute-start | bytes 1277960 | tf_op jit(solution)/shard_map/ppermute | solution.py:349
  10.0 0.8 copy-start.2
  17.7 6.4 %collective-permute-start.1 = (f32[208,128]{1,0:T(8,128)}, f32[208,128]{1,0:T(8,128)S(1)}, u32[]{:S(2)}, u32[]{:S(2)}) collective-permute-start(f32[208,128]{1,0:T(8,128)} %get-tuple-element.30), channel_id=1, source_target_pairs={{0,4},{2,6},{4,0},{6,2},{8,12},{10,14},{12,8},{14,10},{1,5},{3,7},... | collective-permute-start | bytes 319496 | tf_op jit(solution)/shard_map/ppermute | solution.py:349
  20.6 11.4 %collective-permute-start.2 = (f32[208,128]{1,0:T(8,128)}, f32[208,128]{1,0:T(8,128)S(1)}, u32[]{:S(2)}, u32[]{:S(2)}) collective-permute-start(f32[208,128]{1,0:T(8,128)} %get-tuple-element.31), channel_id=1, source_target_pairs={{0,8},{2,10},{4,12},{6,14},{8,0},{10,2},{12,4},{14,6},{1,9},{3,11}... | collective-permute-start | bytes 319496 | tf_op jit(solution)/shard_map/ppermute | solution.py:349
  23.2 8.8 %collective-permute-start.3 = (f32[208,128]{1,0:T(8,128)}, f32[208,128]{1,0:T(8,128)S(1)}, u32[]{:S(2)}, u32[]{:S(2)}) collective-permute-start(f32[208,128]{1,0:T(8,128)} %get-tuple-element.32), channel_id=1, source_target_pairs={{0,12},{2,14},{4,8},{6,10},{8,4},{10,6},{12,0},{14,2},{1,13},{3,15... | collective-permute-start | bytes 319496 | tf_op jit(solution)/shard_map/ppermute | solution.py:349
  24.1 7.9 %copy-start.3 = (f32[208,128]{1,0:T(8,128)}, f32[208,128]{1,0:T(8,128)S(1)}, u32[]{:S(2)}) copy-start(f32[208,128]{1,0:T(8,128)S(1)} %collective-permute-done.1.refs_1_) | copy-start | bytes 319492
  32.0 0.6 copy-start.4
  32.0 0.7 copy-start.5
  34.7 3.8 %collective-permute-start.4 = (f32[8,128]{1,0:T(8,128)}, f32[8,128]{1,0:T(8,128)S(1)}, u32[]{:S(2)}, u32[]{:S(2)}) collective-permute-start(f32[8,128]{1,0:T(8,128)} %get-tuple-element.33), channel_id=1, source_target_pairs={{0,16},{16,0},{1,17},{17,1},{2,18},{18,2},{3,19},{19,3},{4,20},{20... | collective-permute-start | bytes 12296 | tf_op jit(solution)/shard_map/ppermute | solution.py:376
  39.2 3.6 %collective-permute-start.5 = (f32[8,128]{1,0:T(8,128)S(1)}, f32[8,128]{1,0:T(8,128)S(1)}, u32[]{:S(2)}, u32[]{:S(2)}) collective-permute-start(f32[8,128]{1,0:T(8,128)S(1)} %max.6), channel_id=1, source_target_pairs={{0,1},{1,0},{2,3},{3,2},{4,5},{5,4},{6,7},{7,6},{8,9},{9,8},{10,11... | collective-permute-start | bytes 12296 | tf_op jit(solution)/shard_map/ppermute | solution.py:376
  47.0 7.5 %collective-permute-start.7 = (f32[208,128]{1,0:T(8,128)}, f32[208,128]{1,0:T(8,128)S(1)}, u32[]{:S(2)}, u32[]{:S(2)}) collective-permute-start(f32[208,128]{1,0:T(8,128)} %newton_schulz.1), channel_id=1, source_target_pairs={{0,8},{2,10},{4,12},{6,14},{8,0},{10,2},{12,4},{14,6},{1,9},{3,11}... | collective-permute-start | bytes 319496 | tf_op jit(solution)/shard_map/ppermute | solution.py:349
  49.9 6.8 %collective-permute-start.8 = (f32[208,128]{1,0:T(8,128)}, f32[208,128]{1,0:T(8,128)S(1)}, u32[]{:S(2)}, u32[]{:S(2)}) collective-permute-start(f32[208,128]{1,0:T(8,128)} %newton_schulz.1), channel_id=1, source_target_pairs={{0,12},{2,14},{4,8},{6,10},{8,4},{10,6},{12,0},{14,2},{1,13},{3,15... | collective-permute-start | bytes 319496 | tf_op jit(solution)/shard_map/ppermute | solution.py:349
  51.2 6.1 %collective-permute-start.6 = (f32[208,128]{1,0:T(8,128)}, f32[208,128]{1,0:T(8,128)S(1)}, u32[]{:S(2)}, u32[]{:S(2)}) collective-permute-start(f32[208,128]{1,0:T(8,128)} %newton_schulz.1), channel_id=1, source_target_pairs={{0,4},{2,6},{4,0},{6,2},{8,12},{10,14},{12,8},{14,10},{1,5},{3,7},... | collective-permute-start | bytes 319496 | tf_op jit(solution)/shard_map/ppermute | solution.py:349
  58.2 22.6 %collective-permute-start.9 = (f32[4,208,128]{2,1,0:T(8,128)S(1)}, f32[4,208,128]{2,1,0:T(8,128)S(1)}, u32[]{:S(2)}, u32[]{:S(2)}) collective-permute-start(f32[4,208,128]{2,1,0:T(8,128)S(1)} %pad_maximum_fusion.factor_ref), channel_id=1, source_target_pairs={{0,2},{2,0},{4,6},{6,4},{8,10},{10,8},{12,14},{14,12},{1,3},{3,1},... | collective-permute-start | bytes 1277960 | tf_op jit(solution)/shard_map/ppermute | solution.py:349
  69.8 4.2 %copy-start = (s32[4]{0:T(128)S(1)}, s32[4]{0:T(128)}, u32[]{:S(2)}) copy-start(s32[4]{0:T(128)} %get-tuple-element.37.group_ref) | copy-start | bytes 52
  74.1 6.7 %copy-start.1 = (s32[4]{0:T(128)S(1)}, s32[4]{0:T(128)}, u32[]{:S(2)}) copy-start(s32[4]{0:T(128)} %get-tuple-element.36.group_ref) | copy-start | bytes 52

commit v2 on v1

--- a/solution.py
+++ b/solution.py
@@ -360,7 +360,8 @@
     mine = jnp.stack([place ^ (2 * k) for k in range(chips)]).astype(jnp.int32)
     theirs = mine ^ 1
     groups = heads // per
-    early = groups - groups // 3
+    late = groups - groups // 4
+    begun = late - len(axis_sizes)
     for_sibling = local_grams(theirs, gradient, momentum, per)
     from_sibling = swap(for_sibling, 1, devices)
     sums = local_grams(mine, gradient, momentum, per, from_sibling)
@@ -369,12 +370,14 @@
         pieces.append(swap(sums[k], 2 * k, devices))
     gradient, momentum, anchor = lax.optimization_barrier((gradient, momentum, sums[0]))
     pieces[0] = anchor
-    partly = update_momentum(gradient, momentum, per, 0, early)
+    partly = update_momentum(gradient, momentum, per, 0, begun)
     gram, estimate = sum_and_estimate(pieces, probe_vector.reshape(1, width), per)
     for name, size in axis_sizes:
-        others = [
-            lax.ppermute(estimate, name, [(i, (i + k) % size) for i in range(size)]) for k in range(1, size)
-        ]
+        others = []
+        for k in range(1, size):
+            others.append(lax.ppermute(estimate, name, [(i, (i + k) % size) for i in range(size)]))
+        partly = update_momentum(gradient, momentum, per, begun, begun + 1, partly)
+        begun += 1
         for other in others:
             estimate = jnp.maximum(estimate, other)
     factor = newton_schulz(estimate, gram, rows * devices)
@@ -382,7 +385,7 @@
     for k in range(1, chips):
         factors.append(swap(factor, 2 * k, devices))
     gradient, momentum, *partly = lax.optimization_barrier((gradient, momentum, *partly))
-    new_momentum, halves = update_momentum(gradient, momentum, per, early, groups, partly)
+    new_momentum, halves = update_momentum(gradient, momentum, per, late, groups, partly)
     factors = jnp.stack(factors)
     sibling_factors = swap(factors, 1, devices)
     update = apply_factors(mine, factors, halves, per)
@@ -397,7 +400,7 @@
 
     def body(gradient, momentum, probe_vector):
         groups, layers, heads = gradient.shape[:3]
-        if groups == 1 and layers == 1 and heads % devices == 0 and devices > 1 and devices & (devices - 1) == 0:
+        if groups == 1 and layers == 1 and heads % devices == 0 and devices > 4 and devices & (devices - 1) == 0:
             return on_device(gradient, momentum, probe_vector, devices, axis_sizes)
         return on_device_general(gradient, momentum, probe_vector)
 

time: 88 us -> 91 us (1.034)
  Pallas kernels: 48.3 us -> 51.3 us
    pallas_call x2 -> x4, Pallas kernels: 15.8 us -> 18.8 us  [update_momentum(): pl.pallas_call(functools.partial(momentum_kernel, per), name='update_mome...]
  transfers between devices with their start and end apart: 10 -> 10, of which waited for: 8 -> 8; matrix products, arithmetic and copies ran while one was open for 0% -> 0% of each run, Pallas kernels for 26% -> 28%
where the time goes in v2:
time: 91 us; the launch traced here: 90.4 us
  Pallas kernels  51.3 us (56%)
  waiting for transfers between devices  20.7 us (23%)
  starting transfers between devices  13.4 us (15%)
  other arithmetic  2.81 us (3%)
  local copies, waits for them, and re-layouts  1.44 us (2%)
    pallas_call x4, Pallas kernels, update_momentum(): pl.pallas_call(functools.partial(momentum_kernel, per), name='update_mome...  18.8 us
    ppermute x8, waiting for transfers between devices, swap(): lax.ppermute(value, 'col', [(i, i ^ distance) for i in range(devices)])  16.5 us
    pallas_call x2, Pallas kernels, local_grams(): pl.pallas_call(functools.partial(gram_kernel, per), name='local_grams', o...  13.6 us
    pallas_call x2, Pallas kernels, apply_factors(): pl.pallas_call(apply_kernel, name='apply_factors', out_shape=jax.ShapeDty...  13.3 us
    ppermute x8, starting transfers between devices, swap(): lax.ppermute(value, 'col', [(i, i ^ distance) for i in range(devices)])  10.3 us
    ppermute x2, waiting for transfers between devices, on_device(): lax.ppermute(estimate, name, [(i, (i + k) % size) for i in range(size)])  4.29 us
    pallas_call x1, Pallas kernels, newton_schulz(): pl.pallas_call(functools.partial(newton_schulz_kernel, depth), name='newt...  3.63 us
    ppermute x2, starting transfers between devices, on_device(): lax.ppermute(estimate, name, [(i, (i + k) % size) for i in range(size)])  3.13 us
  transfers between devices with their start and end apart: 10, of which 8 were waited for; matrix products, arithmetic and copies ran while one was open for 0% of the time, Pallas kernels for 28%

profile of v2, /device:TPU:0, one launch (start us, length us, event | category | flops | bytes accessed | tf_op | source)
XLA Modules:
  0.0 90.4 jit_solution(13615904196210411856)
XLA Ops:
  0.6 0.6 broadcast_xor_fusion
  1.2 6.7 %local_grams.2 = f32[4,208,128]{2,1,0:T(8,128)} custom-call(s32[4]{0:T(128)} %get-tuple-element.44.group_ref, f32[24,768,128]{2,1,0:T(8,128)} %bitcast.13, f32[24,768,128]{2,1,0:T(8,128)} %bitcast.14, f32[24,768,128]{2,1,0:T(8,128)} %bitcast.15, f32[24,768,128]{2,1,0:T(8,128)} %bitcast.31, f32[24,768,128]{2,1,0:T(8,128)} %bitcast.32, f32[24,768,128]{2,1,0:T(8,128)} %bitcast.33), custom_call_target="tpu_custom_call" | custom-call | flops 1207959552 | bytes 9437184 | tf_op jit(solution)/shard_map/local_grams/pallas_call | solution.py:177
  7.9 0.5 collective-permute-start
  8.4 1.6 %collective-permute-done.refs_6_ = f32[4,208,128]{2,1,0:T(8,128)S(1)} collective-permute-done((f32[4,208,128]{2,1,0:T(8,128)}, f32[4,208,128]{2,1,0:T(8,128)S(1)}, u32[]{:S(2)}, u32[]{:S(2)}) %collective-permute-start) | collective-permute-done | bytes 426016 | tf_op jit(solution)/shard_map/ppermute | solution.py:349
  10.0 0.0 copy-start.2
  10.0 0.8 copy-done.2
  10.8 6.9 %local_grams.3 = (f32[208,128]{1,0:T(8,128)}, f32[208,128]{1,0:T(8,128)}, f32[208,128]{1,0:T(8,128)}, f32[208,128]{1,0:T(8,128)}) custom-call(s32[4]{0:T(128)} %get-tuple-element.45.group_ref, f32[24,768,128]{2,1,0:T(8,128)} %bitcast.16, f32[24,768,128]{2,1,0:T(8,128)} %bitcast.17, f32[24,768,128]{2,1,0:T(8,128)} %bitcast.18, f32[24,768,128]{2,1,0:T(8,128)} %bitcast.34, ...), custom_call_target="tpu_custom_call" | custom-call | flops 1207959552 | bytes 9437184 | tf_op jit(solution)/shard_map/local_grams/pallas_call | solution.py:177
  17.7 2.9 %collective-permute-start.1 = (f32[208,128]{1,0:T(8,128)}, f32[208,128]{1,0:T(8,128)S(1)}, u32[]{:S(2)}, u32[]{:S(2)}) collective-permute-start(f32[208,128]{1,0:T(8,128)} %get-tuple-element.38), channel_id=1, source_target_pairs={{0,4},{2,6},{4,0},{6,2},{8,12},{10,14},{12,8},{14,10},{1,5},{3,7},... | collective-permute-start | bytes 319496 | tf_op jit(solution)/shard_map/ppermute | solution.py:349
  20.6 2.6 %collective-permute-start.2 = (f32[208,128]{1,0:T(8,128)}, f32[208,128]{1,0:T(8,128)S(1)}, u32[]{:S(2)}, u32[]{:S(2)}) collective-permute-start(f32[208,128]{1,0:T(8,128)} %get-tuple-element.39), channel_id=1, source_target_pairs={{0,8},{2,10},{4,12},{6,14},{8,0},{10,2},{12,4},{14,6},{1,9},{3,11}... | collective-permute-start | bytes 319496 | tf_op jit(solution)/shard_map/ppermute | solution.py:349
  23.2 0.0 collective-permute-start.3
  23.2 0.9 collective-permute-done.1.refs_1_
  24.1 0.0 copy-start.3
  24.1 7.9 %collective-permute-done.2.refs_2_ = f32[208,128]{1,0:T(8,128)S(1)} collective-permute-done((f32[208,128]{1,0:T(8,128)}, f32[208,128]{1,0:T(8,128)S(1)}, u32[]{:S(2)}, u32[]{:S(2)}) %collective-permute-start.2) | collective-permute-done | bytes 106528 | tf_op jit(solution)/shard_map/ppermute | solution.py:349
  32.0 0.0 copy-start.4
  32.0 0.0 collective-permute-done.3.refs_3_
  32.0 0.0 copy-start.5
  32.0 0.0 copy-done.3
  32.0 0.6 copy-done.4
  32.6 0.1 copy-done.5
  32.7 2.0 %sum_and_estimate.1 = (f32[3,128,128]{2,1,0:T(8,128)}, f32[8,128]{1,0:T(8,128)}) custom-call(f32[1,128]{1,0:T(1,128)} %bitcast.55, f32[208,128]{1,0:T(8,128)} %get-tuple-element.37.refs_0_, f32[208,128]{1,0:T(8,128)} %copy-done.3, f32[208,128]{1,0:T(8,128)} %copy-done.4, f32[208,128]{1,0:T(8,128)} %copy-done.5), custom_call_target="tpu_custom_call" | custom-call | tf_op jit(solution)/shard_map/sum_and_estimate/pallas_call | solution.py:253
  34.7 1.6 %collective-permute-start.4 = (f32[8,128]{1,0:T(8,128)}, f32[8,128]{1,0:T(8,128)S(1)}, u32[]{:S(2)}, u32[]{:S(2)}) collective-permute-start(f32[8,128]{1,0:T(8,128)} %get-tuple-element.41), channel_id=1, source_target_pairs={{0,16},{16,0},{1,17},{17,1},{2,18},{18,2},{3,19},{19,3},{4,20},{20... | collective-permute-start | bytes 12296 | tf_op jit(solution)/shard_map/ppermute | solution.py:378
  36.2 2.3 %collective-permute-done.4 = f32[8,128]{1,0:T(8,128)S(1)} collective-permute-done((f32[8,128]{1,0:T(8,128)}, f32[8,128]{1,0:T(8,128)S(1)}, u32[]{:S(2)}, u32[]{:S(2)}) %collective-permute-start.4) | collective-permute-done | bytes 4128 | tf_op jit(solution)/shard_map/ppermute | solution.py:378
  38.5 0.7 max.6
  39.2 1.6 %collective-permute-start.5 = (f32[8,128]{1,0:T(8,128)S(1)}, f32[8,128]{1,0:T(8,128)S(1)}, u32[]{:S(2)}, u32[]{:S(2)}) collective-permute-start(f32[8,128]{1,0:T(8,128)S(1)} %max.6), channel_id=1, source_target_pairs={{0,1},{1,0},{2,3},{3,2},{4,5},{5,4},{6,7},{7,6},{8,9},{9,8},{10,11... | collective-permute-start | bytes 12296 | tf_op jit(solution)/shard_map/ppermute | solution.py:378
  40.8 2.0 %collective-permute-done.5 = f32[8,128]{1,0:T(8,128)S(1)} collective-permute-done((f32[8,128]{1,0:T(8,128)S(1)}, f32[8,128]{1,0:T(8,128)S(1)}, u32[]{:S(2)}, u32[]{:S(2)}) %collective-permute-start.5) | collective-permute-done | bytes 4128 | tf_op jit(solution)/shard_map/ppermute | solution.py:378
  42.8 0.6 max.7.estimate_ref
  43.4 3.6 %newton_schulz.1 = f32[208,128]{1,0:T(8,128)} custom-call(f32[8,128]{1,0:T(8,128)} %max.7.estimate_ref, f32[3,128,128]{2,1,0:T(8,128)} %get-tuple-element.42.gram_ref), custom_call_target="tpu_custom_call" | custom-call | tf_op jit(solution)/shard_map/newton_schulz/pallas_call | solution.py:289
  47.0 2.9 %collective-permute-start.7 = (f32[208,128]{1,0:T(8,128)}, f32[208,128]{1,0:T(8,128)S(1)}, u32[]{:S(2)}, u32[]{:S(2)}) collective-permute-start(f32[208,128]{1,0:T(8,128)} %newton_schulz.1), channel_id=1, source_target_pairs={{0,8},{2,10},{4,12},{6,14},{8,0},{10,2},{12,4},{14,6},{1,9},{3,11}... | collective-permute-start | bytes 319496 | tf_op jit(solution)/shard_map/ppermute | solution.py:349
  49.9 1.3 %collective-permute-start.8 = (f32[208,128]{1,0:T(8,128)}, f32[208,128]{1,0:T(8,128)S(1)}, u32[]{:S(2)}, u32[]{:S(2)}) collective-permute-start(f32[208,128]{1,0:T(8,128)} %newton_schulz.1), channel_id=1, source_target_pairs={{0,12},{2,14},{4,8},{6,10},{8,4},{10,6},{12,0},{14,2},{1,13},{3,15... | collective-permute-start | bytes 319496 | tf_op jit(solution)/shard_map/ppermute | solution.py:349
  51.2 0.0 collective-permute-start.6
  51.2 3.3 %collective-permute-done.7 = f32[208,128]{1,0:T(8,128)S(1)} collective-permute-done((f32[208,128]{1,0:T(8,128)}, f32[208,128]{1,0:T(8,128)S(1)}, u32[]{:S(2)}, u32[]{:S(2)}) %collective-permute-start.7) | collective-permute-done | bytes 106528 | tf_op jit(solution)/shard_map/ppermute | solution.py:349
  54.5 2.2 %collective-permute-done.8 = f32[208,128]{1,0:T(8,128)S(1)} collective-permute-done((f32[208,128]{1,0:T(8,128)}, f32[208,128]{1,0:T(8,128)S(1)}, u32[]{:S(2)}, u32[]{:S(2)}) %collective-permute-start.8) | collective-permute-done | bytes 106528 | tf_op jit(solution)/shard_map/ppermute | solution.py:349
  56.7 0.5 collective-permute-done.6
  57.3 0.9 %pad_maximum_fusion.factor_ref = f32[4,208,128]{2,1,0:T(8,128)S(1)} fusion(f32[1,208,128]{2,1,0:T(8,128)S(1)} %bitcast.53, f32[1,208,128]{2,1,0:T(8,128)S(1)} %bitcast.52, f32[1,208,128]{2,1,0:T(8,128)S(1)} %bitcast.54, f32[1,208,128]{2,1,0:T(8,128)} %bitcast.51), kind=kLoop, calls=%fused_computation | loop fusion | flops 319488 | bytes 851968 | tf_op jit(solution)/shard_map/stack | solution.py:389
  58.2 0.1 collective-permute-start.9
  58.3 7.9 %update_momentum.4 = (f32[24,768,128]{2,1,0:T(8,128)}, bf16[24,768,256]{2,1,0:T(8,128)(2,1)}) custom-call(f32[24,768,128]{2,1,0:T(8,128)} %bitcast.19, f32[24,768,128]{2,1,0:T(8,128)} %bitcast.20, f32[24,768,128]{2,1,0:T(8,128)} %bitcast.21, f32[24,768,128]{2,1,0:T(8,128)} %bitcast.37, f32[24,768,128]{2,1,0:T(8,128)} %bitcast.38, f32[24,768,128]{2,1,0:T(8,128)} %bitcast.39), custom_call_target="tpu_custom_call" | custom-call | flops 471859200 | bytes 18874368 | tf_op jit(solution)/shard_map/update_momentum/pallas_call | solution.py:214
  66.1 3.4 %update_momentum.5 = (f32[24,768,128]{2,1,0:T(8,128)}, bf16[24,768,256]{2,1,0:T(8,128)(2,1)}) custom-call(f32[24,768,128]{2,1,0:T(8,128)} %bitcast.22, f32[24,768,128]{2,1,0:T(8,128)} %bitcast.23, f32[24,768,128]{2,1,0:T(8,128)} %bitcast.24, f32[24,768,128]{2,1,0:T(8,128)} %bitcast.40, ...), custom_call_target="tpu_custom_call", output_to_operand_aliasing={{0}: (6, {}), {1}: (7, {})} | custom-call | flops 117964800 | bytes 4718592 | tf_op jit(solution)/shard_map/update_momentum/pallas_call | solution.py:214
  69.5 3.4 %update_momentum.6 = (f32[24,768,128]{2,1,0:T(8,128)}, bf16[24,768,256]{2,1,0:T(8,128)(2,1)}) custom-call(f32[24,768,128]{2,1,0:T(8,128)} %bitcast.25, f32[24,768,128]{2,1,0:T(8,128)} %bitcast.26, f32[24,768,128]{2,1,0:T(8,128)} %bitcast.27, f32[24,768,128]{2,1,0:T(8,128)} %bitcast.43, ...), custom_call_target="tpu_custom_call", output_to_operand_aliasing={{0}: (6, {}), {1}: (7, {})} | custom-call | flops 117964800 | bytes 4718592 | tf_op jit(solution)/shard_map/update_momentum/pallas_call | solution.py:214
  72.8 0.0 copy-start
  72.8 4.2 %update_momentum.7 = (f32[24,768,128]{2,1,0:T(8,128)}, bf16[24,768,256]{2,1,0:T(8,128)(2,1)}) custom-call(f32[24,768,128]{2,1,0:T(8,128)} %bitcast.28, f32[24,768,128]{2,1,0:T(8,128)} %bitcast.29, f32[24,768,128]{2,1,0:T(8,128)} %bitcast.30, f32[24,768,128]{2,1,0:T(8,128)} %bitcast.46, ...), custom_call_target="tpu_custom_call", output_to_operand_aliasing={{0}: (6, {}), {1}: (7, {})} | custom-call | flops 235929600 | bytes 9437184 | tf_op jit(solution)/shard_map/update_momentum/pallas_call | solution.py:214
  77.0 0.0 copy-done
  77.0 0.0 copy-start.1
  77.1 6.7 %apply_factors.2.refs_3_ = f32[24,768,128]{2,1,0:T(8,128)} custom-call(s32[4]{0:T(128)S(1)} %copy-done, f32[4,208,128]{2,1,0:T(8,128)S(1)} %pad_maximum_fusion.factor_ref, bf16[24,768,256]{2,1,0:T(8,128)(2,1)} %get-tuple-element.43.refs_0_.refs_1_.refs_2_, bf16[24,768,256]{2,1,0:T(8,128)(2,1)} %get-tuple-element.43.refs_0_.refs_1_.refs_2_, ...), custom_call_target="tpu_custom_call" | custom-call | flops 1207959552 | bytes 9437184 | tf_op jit(solution)/shard_map/apply_factors/pallas_call | solution.py:328
  83.7 0.0 collective-permute-done.9.factor_ref
  83.7 0.0 copy-done.1
  83.7 6.7 %apply_factors.3 = f32[24,768,128]{2,1,0:T(8,128)} custom-call(s32[4]{0:T(128)S(1)} %copy-done.1, f32[4,208,128]{2,1,0:T(8,128)S(1)} %collective-permute-done.9.factor_ref, bf16[24,768,256]{2,1,0:T(8,128)(2,1)} %get-tuple-element.43.refs_0_.refs_1_.refs_2_, ...), custom_call_target="tpu_custom_call", output_to_operand_aliasing={{}: (5, {})} | custom-call | flops 1207959552 | bytes 9437184 | tf_op jit(solution)/shard_map/apply_factors/pallas_call | solution.py:328
Async XLA Ops:
  7.9 2.1 %collective-permute-start = (f32[4,208,128]{2,1,0:T(8,128)}, f32[4,208,128]{2,1,0:T(8,128)S(1)}, u32[]{:S(2)}, u32[]{:S(2)}) collective-permute-start(f32[4,208,128]{2,1,0:T(8,128)} %local_grams.2), channel_id=1, source_target_pairs={{0,2},{2,0},{4,6},{6,4},{8,10},{10,8},{12,14},{14,12},{1,3},{3,1},... | collective-permute-start | bytes 1277960 | tf_op jit(solution)/shard_map/ppermute | solution.py:349
  10.0 0.8 copy-start.2
  17.7 6.4 %collective-permute-start.1 = (f32[208,128]{1,0:T(8,128)}, f32[208,128]{1,0:T(8,128)S(1)}, u32[]{:S(2)}, u32[]{:S(2)}) collective-permute-start(f32[208,128]{1,0:T(8,128)} %get-tuple-element.38), channel_id=1, source_target_pairs={{0,4},{2,6},{4,0},{6,2},{8,12},{10,14},{12,8},{14,10},{1,5},{3,7},... | collective-permute-start | bytes 319496 | tf_op jit(solution)/shard_map/ppermute | solution.py:349
  20.6 11.4 %collective-permute-start.2 = (f32[208,128]{1,0:T(8,128)}, f32[208,128]{1,0:T(8,128)S(1)}, u32[]{:S(2)}, u32[]{:S(2)}) collective-permute-start(f32[208,128]{1,0:T(8,128)} %get-tuple-element.39), channel_id=1, source_target_pairs={{0,8},{2,10},{4,12},{6,14},{8,0},{10,2},{12,4},{14,6},{1,9},{3,11}... | collective-permute-start | bytes 319496 | tf_op jit(solution)/shard_map/ppermute | solution.py:349
  23.2 8.8 %collective-permute-start.3 = (f32[208,128]{1,0:T(8,128)}, f32[208,128]{1,0:T(8,128)S(1)}, u32[]{:S(2)}, u32[]{:S(2)}) collective-permute-start(f32[208,128]{1,0:T(8,128)} %get-tuple-element.40), channel_id=1, source_target_pairs={{0,12},{2,14},{4,8},{6,10},{8,4},{10,6},{12,0},{14,2},{1,13},{3,15... | collective-permute-start | bytes 319496 | tf_op jit(solution)/shard_map/ppermute | solution.py:349
  24.1 7.9 %copy-start.3 = (f32[208,128]{1,0:T(8,128)}, f32[208,128]{1,0:T(8,128)S(1)}, u32[]{:S(2)}) copy-start(f32[208,128]{1,0:T(8,128)S(1)} %collective-permute-done.1.refs_1_) | copy-start | bytes 319492
  32.0 0.6 copy-start.4
  32.0 0.7 copy-start.5
  34.7 3.8 %collective-permute-start.4 = (f32[8,128]{1,0:T(8,128)}, f32[8,128]{1,0:T(8,128)S(1)}, u32[]{:S(2)}, u32[]{:S(2)}) collective-permute-start(f32[8,128]{1,0:T(8,128)} %get-tuple-element.41), channel_id=1, source_target_pairs={{0,16},{16,0},{1,17},{17,1},{2,18},{18,2},{3,19},{19,3},{4,20},{20... | collective-permute-start | bytes 12296 | tf_op jit(solution)/shard_map/ppermute | solution.py:378
  39.2 3.6 %collective-permute-start.5 = (f32[8,128]{1,0:T(8,128)S(1)}, f32[8,128]{1,0:T(8,128)S(1)}, u32[]{:S(2)}, u32[]{:S(2)}) collective-permute-start(f32[8,128]{1,0:T(8,128)S(1)} %max.6), channel_id=1, source_target_pairs={{0,1},{1,0},{2,3},{3,2},{4,5},{5,4},{6,7},{7,6},{8,9},{9,8},{10,11... | collective-permute-start | bytes 12296 | tf_op jit(solution)/shard_map/ppermute | solution.py:378
  47.0 7.5 %collective-permute-start.7 = (f32[208,128]{1,0:T(8,128)}, f32[208,128]{1,0:T(8,128)S(1)}, u32[]{:S(2)}, u32[]{:S(2)}) collective-permute-start(f32[208,128]{1,0:T(8,128)} %newton_schulz.1), channel_id=1, source_target_pairs={{0,8},{2,10},{4,12},{6,14},{8,0},{10,2},{12,4},{14,6},{1,9},{3,11}... | collective-permute-start | bytes 319496 | tf_op jit(solution)/shard_map/ppermute | solution.py:349
  49.9 6.8 %collective-permute-start.8 = (f32[208,128]{1,0:T(8,128)}, f32[208,128]{1,0:T(8,128)S(1)}, u32[]{:S(2)}, u32[]{:S(2)}) collective-permute-start(f32[208,128]{1,0:T(8,128)} %newton_schulz.1), channel_id=1, source_target_pairs={{0,12},{2,14},{4,8},{6,10},{8,4},{10,6},{12,0},{14,2},{1,13},{3,15... | collective-permute-start | bytes 319496 | tf_op jit(solution)/shard_map/ppermute | solution.py:349
  51.2 6.1 %collective-permute-start.6 = (f32[208,128]{1,0:T(8,128)}, f32[208,128]{1,0:T(8,128)S(1)}, u32[]{:S(2)}, u32[]{:S(2)}) collective-permute-start(f32[208,128]{1,0:T(8,128)} %newton_schulz.1), channel_id=1, source_target_pairs={{0,4},{2,6},{4,0},{6,2},{8,12},{10,14},{12,8},{14,10},{1,5},{3,7},... | collective-permute-start | bytes 319496 | tf_op jit(solution)/shard_map/ppermute | solution.py:349
  58.2 25.5 %collective-permute-start.9 = (f32[4,208,128]{2,1,0:T(8,128)S(1)}, f32[4,208,128]{2,1,0:T(8,128)S(1)}, u32[]{:S(2)}, u32[]{:S(2)}) collective-permute-start(f32[4,208,128]{2,1,0:T(8,128)S(1)} %pad_maximum_fusion.factor_ref), channel_id=1, source_target_pairs={{0,2},{2,0},{4,6},{6,4},{8,10},{10,8},{12,14},{14,12},{1,3},{3,1},... | collective-permute-start | bytes 1277960 | tf_op jit(solution)/shard_map/ppermute | solution.py:349
  72.8 4.2 %copy-start = (s32[4]{0:T(128)S(1)}, s32[4]{0:T(128)}, u32[]{:S(2)}) copy-start(s32[4]{0:T(128)} %get-tuple-element.45.group_ref) | copy-start | bytes 52
  77.0 6.7 %copy-start.1 = (s32[4]{0:T(128)S(1)}, s32[4]{0:T(128)}, u32[]{:S(2)}) copy-start(s32[4]{0:T(128)} %get-tuple-element.44.group_ref) | copy-start | bytes 52
